TPU v7x, 32 devices: a whole 2x2x4 slice. The times are simulated.
32 devices in a mesh: gz: 2 (over x), gy: 4 (over y, core), gx: 4 (over z).
Axes of the slice: x: 2, y: 2, z: 4, core: 2. Of those that a mesh axis runs over, the one named last changes fastest.
Arguments:
- density: float32 [32, 64, 256], P('gx', 'gy', 'gz'), may hold values from 0.05 to 0.95
- spread: float32 [32, 64, 256], P('gx', 'gy', 'gz'), may hold values from 0.05 to 0.3
- sensitivities: float32 [9, 32, 64, 256], P(None, 'gx', 'gy', 'gz'), may hold values from -180 to 180, as said below
- violation: float32 [9], replicated, may hold values from -0.05 to 0.15
- multipliers_start: float32 [9], replicated, may hold values from 0.1 to 10
Outputs:
- new_density: float32 [32, 64, 256], P('gx', 'gy', 'gz')
- multipliers: float32 [9], replicated
Inputs may be any that keep to these rules, and one draw needn't show every extreme that they name: `sensitivities`: Real-valued, independent from voxel to voxel.
All inputs are finite; a program needn't handle non-finite values.
Results may differ from a plain program's by a relative error of at most 0.0003.
Values sent between devices are 32-bit elements; how exact they have to be, the bound alone decides.
A program may use at most 64 MiB of HBM per device.

v0:
```python
import math

import jax
import jax.numpy as jnp
from jax import lax
from jax.sharding import PartitionSpec as P

FIELDS = 9
ITERS = 3


RADIUS = 3.0
RAA = 1e-05
MOVE = 0.9
REG = 0.001
FLOOR = 0.2


def padded_2(block, sides, width):
    for axis, dim in sides:
        count = lax.axis_size(axis)
        forward = [(i, i + 1) for i in range(count - 1)]
        backward = [(target, source) for source, target in forward]
        low = lax.ppermute(
            lax.slice_in_dim(block, block.shape[dim] - width, None, axis=dim), axis, forward
        )
        high = lax.ppermute(lax.slice_in_dim(block, 0, width, axis=dim), axis, backward)
        block = jnp.concatenate([low, block, high], axis=dim)
    return block


def smooth(padded, nx, ny, nz):
    total = None
    for a in (-1, 0, 1):
        for b in (-1, 0, 1):
            for c in (-1, 0, 1):
                weight = RADIUS - math.sqrt(a * a + b * b + c * c)
                piece = padded[..., 1 + a : 1 + a + nx, 1 + b : 1 + b + ny, 1 + c : 1 + c + nz]
                total = weight * piece if total is None else total + weight * piece
    return total


def inside(index, extent, count):
    first = (index > 0).astype(jnp.float32)
    last = (index < extent - 1).astype(jnp.float32)
    return jnp.concatenate([first[None], jnp.ones((count,), jnp.float32), last[None]])


def totals(gradient_part, schur_part):
    return lax.psum((gradient_part, schur_part), ("gz", "gy", "gx"))


def shards(density, spread, sensitivities, violation, multipliers_start):
    nx, ny, nz = density.shape
    padded = padded_2(sensitivities, (("gz", 3), ("gy", 2), ("gx", 1)), 1)
    mask_x = inside(lax.axis_index("gx"), lax.axis_size("gx"), nx)
    mask_y = inside(lax.axis_index("gy"), lax.axis_size("gy"), ny)
    mask_z = inside(lax.axis_index("gz"), lax.axis_size("gz"), nz)
    valid = mask_x[:, None, None] * mask_y[None, :, None] * mask_z[None, None, :]
    denom = smooth(valid, nx, ny, nz)
    filtered = smooth(padded, nx, ny, nz) / denom[None]
    cells = nx * ny * nz
    dens = density.reshape(-1)
    span = spread.reshape(-1)
    rows = jnp.concatenate(
        [filtered.reshape(FIELDS, cells), jnp.ones((1, cells), jnp.float32)], axis=0
    )
    grow = jnp.maximum(rows, 0.0)
    fall = jnp.maximum(-rows, 0.0)
    square = span * span
    pp = square * (1.001 * grow + 0.001 * fall + RAA)
    qq = square * (0.001 * grow + 1.001 * fall + RAA)
    lower = dens - span
    upper = dens + span
    floor_x = jnp.maximum(0.0, dens - MOVE * span)
    ceil_x = jnp.minimum(1.0, dens + MOVE * span)
    base = (pp[1:] + qq[1:]) / span
    keep = 1.0 - violation
    base_local = jnp.sum(base, axis=1)
    bound = None
    bound = keep * lax.psum(base_local, ("gz", "gy", "gx"))

    def respond(lam):
        weights = jnp.concatenate([jnp.ones((1,), jnp.float32), lam])
        big_p = jnp.dot(weights, pp, precision=lax.Precision.HIGHEST)
        big_q = jnp.dot(weights, qq, precision=lax.Precision.HIGHEST)
        root_p = jnp.sqrt(big_p)
        root_q = jnp.sqrt(big_q)
        moved = (root_p * lower + root_q * upper) / (root_p + root_q)
        return (jnp.clip(moved, floor_x, ceil_x), big_p, big_q)

    lam = multipliers_start
    for step in range(ITERS):
        moved, big_p, big_q = respond(lam)
        above = upper - moved
        below = moved - lower
        values = pp[1:] / above + qq[1:] / below
        slopes = pp[1:] / (above * above) - qq[1:] / (below * below)
        curv = 2.0 * big_p / (above * above * above) + 2.0 * big_q / (below * below * below)
        schur_part = jnp.dot(slopes / curv, slopes.T, precision=lax.Precision.HIGHEST)
        summed, schur = totals(jnp.sum(values, axis=1), schur_part)
        gradient = summed - bound
        shift = REG * jnp.trace(schur) / FIELDS
        system = schur + shift * jnp.eye(FIELDS, dtype=jnp.float32)
        factor = jnp.linalg.cholesky(system)
        delta = jax.scipy.linalg.cho_solve((factor, True), gradient)
        lam = jnp.maximum(lam + delta, FLOOR * lam)
    moved, big_p, big_q = respond(lam)
    return (moved.reshape(nx, ny, nz), lam)


def solution(mesh):
    return jax.shard_map(
        shards,
        mesh=mesh,
        in_specs=(P("gx", "gy", "gz"), P("gx", "gy", "gz"), P(None, "gx", "gy", "gz"), P(), P()),
        out_specs=(P("gx", "gy", "gz"), P()),
        check_vma=False,
    )
```

profile of v0, /device:TPU:0, one launch (start us, length us, event | category | flops | bytes accessed | tf_op | source)
XLA Modules:
  0.0 187.6 jit_solution(5219307162577140861)
XLA Ops:
  0.6 1.5 fusion.136
  2.7 4.9 %collective-permute-start = (f32[9,8,16,1]{2,1,3,0:T(8,128)S(1)}, f32[9,8,16,1]{2,1,3,0:T(8,128)S(1)}, u32[]{:S(2)}, u32[]{:S(2)}) collective-permute-start(f32[9,8,16,1]{2,1,3,0:T(8,128)S(1)} %copy.82), channel_id=1, source_target_pairs={{0,16},{1,17},{2,18},{3,19},{4,20},{5,21},{6,22},{7,23},{8,24},{9,... | collective-permute-start | bytes 13832 | tf_op jit(solution)/shard_map/ppermute | solution.py:24
  8.0 1.3 collective-permute-start.1
  10.5 3.4 %collective-permute-done.1 = f32[9,8,16,1]{2,1,3,0:T(8,128)S(1)} collective-permute-done((f32[9,8,16,1]{2,1,3,0:T(8,128)S(1)}, f32[9,8,16,1]{2,1,3,0:T(8,128)S(1)}, u32[]{:S(2)}, u32[]{:S(2)}) %collective-permute-start.1) | collective-permute-done | bytes 4640 | tf_op jit(solution)/shard_map/ppermute | solution.py:27
  14.5 1.3 collective-permute-start.2
  15.8 1.3 collective-permute-start.3
  17.5 3.2 %collective-permute-done.3 = f32[9,8,1,130]{3,1,2,0:T(8,128)S(1)} collective-permute-done((f32[9,8,1,130]{3,1,2,0:T(8,128)S(1)}, f32[9,8,1,130]{3,1,2,0:T(8,128)S(1)}, u32[]{:S(2)}, u32[]{:S(2)}) %collective-permute-start.3) | collective-permute-done | bytes 37472 | tf_op jit(solution)/shard_map/ppermute | solution.py:27
  20.7 1.0 pad_maximum_fusion.8
  21.7 3.5 %collective-permute-start.4 = (f32[9,1,18,130]{3,2,1,0:T(8,128)S(1)}, f32[9,1,18,130]{3,2,1,0:T(8,128)S(1)}, u32[]{:S(2)}, u32[]{:S(2)}) collective-permute-start(f32[9,1,18,130]{3,2,1,0:T(8,128)S(1)} %copy.60), channel_id=1, source_target_pairs={{0,1},{1,2},{2,3},{4,5},{5,6},{6,7},{8,9},{9,10},{10,11},{12,13},{... | collective-permute-start | bytes 252728 | tf_op jit(solution)/shard_map/ppermute | solution.py:24
  25.3 1.5 collective-permute-start.5
  26.7 1.0 maximum_maximum_fusion.1
  27.7 1.3 collective-permute-done.4
  29.2 4.5 %collective-permute-done.5 = f32[9,1,18,130]{3,2,1,0:T(8,128)S(1)} collective-permute-done((f32[9,1,18,130]{3,2,1,0:T(8,128)S(1)}, f32[9,1,18,130]{3,2,1,0:T(8,128)S(1)}, u32[]{:S(2)}, u32[]{:S(2)}) %collective-permute-start.5) | collective-permute-done | bytes 84272 | tf_op jit(solution)/shard_map/ppermute | solution.py:27
  33.9 2.1 %maximum_maximum_fusion = (f32[9,9,18,130]{3,1,2,0:T(8,128)S(1)}, f32[9,9,18,130]{3,1,2,0:T(8,128)S(1)}) fusion(f32[9,8,1,130]{3,1,2,0:T(8,128)S(1)} %collective-permute-done.3, f32[9,8,16,1]{3,1,2,0:T(8,128)S(1)} %copy.59, f32[9,8,16,128]{3,1,2,0:T(8,128)S(1)} %copy.58, f32[9,8,16,1]{3,1,2,0:T(8,128)S(1)} %copy.57, ...), kind=kLoop, calls=%fused_computation | loop fusion | flops 1895400 | bytes 2358720 | tf_op jit(solution)/shard_map/concatenate | solution.py:28
  36.0 3.1 %fusion.29 = f32[9,8,16,128]{3,1,2,0:T(8,128)S(1)} fusion(f32[9,9,18,130]{3,1,2,0:T(8,128)S(1)} %get-tuple-element.33, f32[9,8,17,130]{3,1,2,0:T(8,128)S(1)} %get-tuple-element.37, f32[9,8,16,1]{3,1,2,0:T(8,128)S(1)} %copy.59, f32[9,8,16,128]{3,1,2,0:T(8,128)S(1)} %copy.58, f32[9,8,16,1]{3,1,2,0:T(8,128)S(1)} %copy.57, ...), kind=kLoop, calls=%fused_computation.47 | loop fusion | flops 8257536 | bytes 15410176 | tf_op jit(solution)/shard_map/div | solution.py:61
  41.9 0.8 fusion.21
  42.8 1.7 fusion.4
  44.5 40.1 %all-reduce.3 = (f32[9,9]{0,1:T(8,128)S(1)}, f32[9]{0:T(128)S(1)}, f32[9]{0:T(128)S(1)}) all-reduce(f32[9,9]{0,1:T(8,128)S(1)} %fusion.4, f32[9]{0:T(128)S(1)} %get-tuple-element.5, f32[9]{0:T(128)S(1)} %get-tuple-element.4), channel_id=1, replica_groups=mesh['gz'=2,'gy'=4,'gx'=4] {'gz','gy','gx'}, use_global_device_ids=true, to_apply=%region_0.0 | all-reduce | flops 99 | bytes 792 | tf_op jit(solution)/shard_map/psum | solution.py:50
  86.0 0.8 cholesky.59
  91.0 1.7 fusion.2
  92.7 40.2 %all-reduce.2 = (f32[9,9]{0,1:T(8,128)S(1)}, f32[9]{0:T(128)S(1)}) all-reduce(f32[9,9]{0,1:T(8,128)S(1)} %fusion.2, f32[9]{0:T(128)S(1)} %add_reduce_fusion.1), channel_id=1, replica_groups=mesh['gz'=2,'gy'=4,'gx'=4] {'gz','gy','gx'}, use_global_device_ids=true, to_apply=%region_8.11 | all-reduce | flops 90 | bytes 720 | tf_op jit(solution)/shard_map/psum | solution.py:50
  134.2 0.8 cholesky.70
  139.3 1.7 fusion
  140.9 40.1 %all-reduce.1 = (f32[9,9]{0,1:T(8,128)S(1)}, f32[9]{0:T(128)S(1)}) all-reduce(f32[9,9]{0,1:T(8,128)S(1)} %fusion, f32[9]{0:T(128)S(1)} %add_reduce_fusion), channel_id=1, replica_groups=mesh['gz'=2,'gy'=4,'gx'=4] {'gz','gy','gx'}, use_global_device_ids=true, to_apply=%region_12.15 | all-reduce | flops 90 | bytes 720 | tf_op jit(solution)/shard_map/psum | solution.py:50
  (89 shorter events, 21.8 us)
Async XLA Ops:
  0.6 9.2 %copy-start = (f32[9,8,16,128]{3,2,1,0:T(8,128)S(1)}, f32[9,8,16,128]{3,2,1,0:T(8,128)}, u32[]{:S(2)}) copy-start(f32[9,8,16,128]{3,2,1,0:T(8,128)} %param.10) | copy-start | bytes 1769476
  2.7 7.4 %collective-permute-start = (f32[9,8,16,1]{2,1,3,0:T(8,128)S(1)}, f32[9,8,16,1]{2,1,3,0:T(8,128)S(1)}, u32[]{:S(2)}, u32[]{:S(2)}) collective-permute-start(f32[9,8,16,1]{2,1,3,0:T(8,128)S(1)} %copy.82), channel_id=1, source_target_pairs={{0,16},{1,17},{2,18},{3,19},{4,20},{5,21},{6,22},{7,23},{8,24},{9,... | collective-permute-start | bytes 13832 | tf_op jit(solution)/shard_map/ppermute | solution.py:24
  8.0 5.9 %collective-permute-start.1 = (f32[9,8,16,1]{2,1,3,0:T(8,128)S(1)}, f32[9,8,16,1]{2,1,3,0:T(8,128)S(1)}, u32[]{:S(2)}, u32[]{:S(2)}) collective-permute-start(f32[9,8,16,1]{2,1,3,0:T(8,128)S(1)} %copy.83), channel_id=1, source_target_pairs={{16,0},{17,1},{18,2},{19,3},{20,4},{21,5},{22,6},{23,7},{24,8},{25... | collective-permute-start | bytes 13832 | tf_op jit(solution)/shard_map/ppermute | solution.py:27
  10.0 7.5 %copy-start.1 = (f32[8,16,128]{2,1,0:T(8,128)S(1)}, f32[8,16,128]{2,1,0:T(8,128)}, u32[]{:S(2)}) copy-start(f32[8,16,128]{2,1,0:T(8,128)} %param.9) | copy-start | bytes 196612
  14.5 3.0 %collective-permute-start.2 = (f32[9,8,1,130]{3,1,2,0:T(8,128)S(1)}, f32[9,8,1,130]{3,1,2,0:T(8,128)S(1)}, u32[]{:S(2)}, u32[]{:S(2)}) collective-permute-start(f32[9,8,1,130]{3,1,2,0:T(8,128)S(1)} %get-tuple-element.38), channel_id=1, source_target_pairs={{0,4},{4,8},{8,12},{1,5},{5,9},{9,13},{2,6},{6,10},{10,14},{3,7},{... | collective-permute-start | bytes 112328 | tf_op jit(solution)/shard_map/ppermute | solution.py:24
  15.8 4.9 %collective-permute-start.3 = (f32[9,8,1,130]{3,1,2,0:T(8,128)S(1)}, f32[9,8,1,130]{3,1,2,0:T(8,128)S(1)}, u32[]{:S(2)}, u32[]{:S(2)}) collective-permute-start(f32[9,8,1,130]{3,1,2,0:T(8,128)S(1)} %get-tuple-element.39), channel_id=1, source_target_pairs={{4,0},{8,4},{12,8},{5,1},{9,5},{13,9},{6,2},{10,6},{14,10},{7,3},{... | collective-permute-start | bytes 112328 | tf_op jit(solution)/shard_map/ppermute | solution.py:27
  21.7 7.3 %collective-permute-start.4 = (f32[9,1,18,130]{3,2,1,0:T(8,128)S(1)}, f32[9,1,18,130]{3,2,1,0:T(8,128)S(1)}, u32[]{:S(2)}, u32[]{:S(2)}) collective-permute-start(f32[9,1,18,130]{3,2,1,0:T(8,128)S(1)} %copy.60), channel_id=1, source_target_pairs={{0,1},{1,2},{2,3},{4,5},{5,6},{6,7},{8,9},{9,10},{10,11},{12,13},{... | collective-permute-start | bytes 252728 | tf_op jit(solution)/shard_map/ppermute | solution.py:24
  25.3 8.4 %collective-permute-start.5 = (f32[9,1,18,130]{3,2,1,0:T(8,128)S(1)}, f32[9,1,18,130]{3,2,1,0:T(8,128)S(1)}, u32[]{:S(2)}, u32[]{:S(2)}) collective-permute-start(f32[9,1,18,130]{3,2,1,0:T(8,128)S(1)} %copy.67), channel_id=1, source_target_pairs={{1,0},{2,1},{3,2},{5,4},{6,5},{7,6},{9,8},{10,9},{11,10},{13,12},{... | collective-permute-start | bytes 252728 | tf_op jit(solution)/shard_map/ppermute | solution.py:27
  39.3 1.2 copy-start.3
  40.0 1.8 copy-start.2
  42.8 46.0 %copy-start.5 = (f32[9]{0:T(128)S(1)}, f32[9]{0:T(128)}, u32[]{:S(2)}) copy-start(f32[9]{0:T(128)} %param.11) | copy-start | bytes 112
  185.6 2.0 %copy-start.4 = (f32[9]{0:T(128)}, f32[9]{0:T(128)S(1)}, u32[]{:S(2)}) copy-start(f32[9]{0:T(128)S(1)} %fusion.11) | copy-start | bytes 112
where the time goes:
time: 188 us
  blocking collectives  120 us (64%)
  other arithmetic  21.8 us (12%)
  starting transfers between devices  13.7 us (7%)
  waiting for transfers between devices  12.4 us (7%)
  matrix products  11 us (6%)
  local copies, waits for them, and re-layouts  5.18 us (3%)
  between operations  3.06 us (2%)
    psum x3, blocking collectives, totals(): return lax.psum((gradient_part, schur_part), ('gz', 'gy', 'gx'))  120 us
    ppermute x3, waiting for transfers between devices, padded_2(): lax.ppermute(lax.slice_in_dim(block, 0, width, axis=dim), axis, backward)  11.1 us
    ppermute x3, starting transfers between devices, padded_2(): lax.ppermute(lax.slice_in_dim(block, block.shape[dim] - width, None, axis...  9.67 us
    dot_general x3, matrix products, shards(): jnp.dot(slopes / curv, slopes.T, precision=lax.Precision.HIGHEST)  5.02 us
    another operation x9, other arithmetic, shards(): factor = jnp.linalg.cholesky(system)  4.45 us
    ppermute x3, starting transfers between devices, padded_2(): lax.ppermute(lax.slice_in_dim(block, 0, width, axis=dim), axis, backward)  4.06 us
    another operation x6, other arithmetic, shards(): delta = jax.scipy.linalg.cho_solve((factor, True), gradient)  4.03 us
  transfers between devices with their start and end apart: 6, of which 4 were waited for; matrix products, arithmetic and copies ran while one was open for 2% of the time, Pallas kernels for 0%

commit v1 on v0

v1 whole, which is shorter than its diff:
```python
import functools
import math

import jax
import jax.numpy as jnp
from jax import lax
from jax.experimental import pallas as pl
from jax.experimental.pallas import tpu as pltpu
from jax.sharding import PartitionSpec as P

FIELDS = 9
ITERS = 3

RADIUS = 3.0
RAA = 1e-05
MOVE = 0.9
REG = 0.001
FLOOR = 0.2

W0 = RADIUS
W1 = RADIUS - 1.0
W2 = RADIUS - math.sqrt(2.0)
W3 = RADIUS - math.sqrt(3.0)

SUB, LANE = 8, 128
AXES = ("gz", "gy", "gx")
SUMS = FIELDS + FIELDS * (FIELDS + 1) // 2
ROWS = SUMS + FIELDS
MESH = pl.DeviceIdType.MESH


def plan(shape):
    total = math.prod(shape[a] for a in AXES)
    if total <= 32:
        return (AXES,)
    return tuple((a,) for a in AXES)


def offsets(axes, shape):
    out = [()]
    for a in axes:
        out = [o + (d,) for o in out for d in range(shape[a])]
    return [o for o in out if any(o)]


def body(shape, dims, dens_ref, span_ref, sens_ref, viol_ref, lam0_ref, out_ref, lam_out,
         pad, ypack, yrecv, cpack, crecv, zsum, zpack, zrecv, mid, invden, pp, qq, slope, scaled,
         acc, wide, lam, part, *rest):
    stages = plan(shape)
    recvs = rest[: len(stages)]
    load_sem, send_sem, recv_sem, sum_send, sum_recv = rest[len(stages):]
    nx, ny, nz = dims
    tiles = ny // SUB
    chunks = nx * tiles
    me = {a: lax.axis_index(a) for a in AXES}

    load = pltpu.make_async_copy(
        sens_ref, pad.at[:, 1 : nx + 1, SUB : SUB + ny, :], load_sem
    )
    load.start()

    partners = set()
    for axes in stages:
        for o in offsets(axes, shape):
            partners.add(tuple(dict(zip(axes, o)).get(a, 0) for a in AXES))
    for dz, dy, dx in [(dz, 0, 0) for dz in (-1, 1)] + [
        (0, dy, dx) for dy in (-1, 0, 1) for dx in (-1, 0, 1)
    ]:
        o = tuple(d % shape[a] for a, d in zip(AXES, (dz, dy, dx)))
        if any(o):
            partners.add(o)
    partners = sorted(partners)
    barrier = pltpu.get_barrier_semaphore()
    for o in partners:
        target = {a: lax.rem(me[a] + d, shape[a]) for a, d in zip(AXES, o)}
        pl.semaphore_signal(barrier, inc=1, device_id=target, device_id_type=MESH)

    has = {}
    for a in AXES:
        has[a, -1] = me[a] > 0
        has[a, 1] = me[a] < shape[a] - 1

    lane = lax.broadcasted_iota(jnp.int32, (SUB, LANE), 1)
    row = lax.broadcasted_iota(jnp.int32, (SUB, LANE), 0)
    zero = jnp.zeros((SUB, LANE), jnp.float32)

    for i, sx in enumerate((1, -1)):
        @pl.when(jnp.logical_not(has["gx", -sx]))
        def _(i=i):
            pad[:, i * (nx + 1), SUB : SUB + ny, :] = jnp.zeros((FIELDS, ny, LANE), jnp.float32)
    for i, sy in enumerate((1, -1)):
        @pl.when(jnp.logical_not(has["gy", -sy]))
        def _(i=i):
            yrecv[i] = jnp.zeros((FIELDS, nx, LANE), jnp.float32)
    for i, sz in enumerate((1, -1)):
        @pl.when(jnp.logical_not(has["gz", -sz]))
        def _(i=i):
            zrecv[i] = jnp.zeros(zrecv.shape[1:], jnp.float32)
    corners = [(sx, sy) for sx in (1, -1) for sy in (1, -1)]
    for i, (sx, sy) in enumerate(corners):
        @pl.when(jnp.logical_not(jnp.logical_and(has["gx", -sx], has["gy", -sy])))
        def _(i=i):
            crecv[i] = jnp.zeros((FIELDS, 1, LANE), jnp.float32)
    zsum[...] = jnp.zeros(zsum.shape, jnp.float32)

    def count(a, index, extent):
        low = jnp.where(jnp.logical_and(me[a] == 0, index == 0), 0.0, 1.0)
        high = jnp.where(jnp.logical_and(me[a] == shape[a] - 1, index == extent - 1), 0.0, 1.0)
        return low + high
    cz = count("gz", lane, nz)
    for x in range(nx):
        cx = count("gx", jnp.full((SUB, LANE), x, jnp.int32), nx)
        for t in range(tiles):
            cy = count("gy", row + t * SUB, ny)
            den = W0 + W1 * (cx + cy + cz) + W2 * (cx * cy + cy * cz + cx * cz) + W3 * (cx * cy * cz)
            k = x * tiles + t
            invden[k] = 1.0 / den

    load.wait()

    def gather(f, carry):
        for i, y in enumerate((SUB + ny - 1, SUB)):
            for x in range(nx):
                ypack[i, f, x : x + 1, :] = pad[f, x + 1, y : y + 1, :]
        for i, (sx, sy) in enumerate(corners):
            x = nx if sx > 0 else 1
            y = SUB + ny - 1 if sy > 0 else SUB
            cpack[i, f] = pad[f, x, y : y + 1, :]
        return carry
    lax.fori_loop(0, FIELDS, gather, 0)

    pl.semaphore_wait(barrier, len(partners))

    def at(**moves):
        return {a: me[a] + d for a, d in moves.items()}

    moves = []
    for i, sx in enumerate((1, -1)):
        copy = pltpu.make_async_remote_copy(
            src_ref=pad.at[:, nx if sx > 0 else 1, SUB : SUB + ny, :],
            dst_ref=pad.at[:, 0 if sx > 0 else nx + 1, SUB : SUB + ny, :],
            send_sem=send_sem.at[i], recv_sem=recv_sem.at[i],
            device_id=at(gx=sx), device_id_type=MESH)
        moves.append((has["gx", sx], has["gx", -sx], copy))
    for i, (sx, sy) in enumerate(corners):
        copy = pltpu.make_async_remote_copy(
            src_ref=cpack.at[i], dst_ref=crecv.at[i],
            send_sem=send_sem.at[4 + i], recv_sem=recv_sem.at[4 + i],
            device_id=at(gx=sx, gy=sy), device_id_type=MESH)
        moves.append((jnp.logical_and(has["gx", sx], has["gy", sy]),
                      jnp.logical_and(has["gx", -sx], has["gy", -sy]), copy))
    for i, sy in enumerate((1, -1)):
        copy = pltpu.make_async_remote_copy(
            src_ref=ypack.at[i], dst_ref=yrecv.at[i],
            send_sem=send_sem.at[2 + i], recv_sem=recv_sem.at[2 + i],
            device_id=at(gy=sy), device_id_type=MESH)
        moves.append((has["gy", sy], has["gy", -sy], copy))
    for send, _, copy in moves:
        pl.when(send)(copy.start)
    for _, receive, copy in moves:
        pl.when(receive)(copy.wait_recv)

    ends = jnp.logical_or(lane == 0, lane == LANE - 1)

    def smooth(f, carry):
        for i, y in enumerate((SUB - 1, SUB + ny)):
            for x in range(nx):
                pad[f, x + 1, y : y + 1, :] = yrecv[i, f, x : x + 1, :]
        for i, (sx, sy) in enumerate(corners):
            pad[f, 0 if sx > 0 else nx + 1, (SUB - 1 if sy > 0 else SUB + ny) : (SUB if sy > 0 else SUB + ny + 1), :] = crecv[i, f]
        packed = zero
        for t in range(tiles):
            y = SUB + t * SUB
            mids, sides = [], []
            for p in range(nx + 2):
                mids.append(pad[f, p, y : y + SUB, :])
                sides.append(pad[f, p, y - 1 : y - 1 + SUB, :] + pad[f, p, y + 1 : y + 1 + SUB, :])
            for x in range(nx):
                k = x * tiles + t
                near = sides[x + 1] + (mids[x] + mids[x + 2])
                far = sides[x] + sides[x + 2]
                s0 = W0 * mids[x + 1] + W1 * near + W2 * far
                s1 = W1 * mids[x + 1] + W2 * near + W3 * far
                up = pltpu.roll(s1, 1, 1)
                down = pltpu.roll(s1, LANE - 1, 1)
                mid[f, k] = s0 + jnp.where(lane == 0, 0.0, up) + jnp.where(lane == LANE - 1, 0.0, down)
                edge = jnp.where(lane == 0, up, down)
                if k:
                    edge = pltpu.roll(edge, 2 * k, 1)
                here = jnp.logical_or(lane == 2 * k, lane == (2 * k - 1) % LANE)
                packed = jnp.where(here, edge, packed)
        zsum[f // per] += pltpu.roll(packed, (f % per) * (2 * chunks), 1)
        return carry
    per = LANE // (2 * chunks)
    lax.fori_loop(0, FIELDS, smooth, 0)

    even = (lane % 2) == 0
    for g in range(zsum.shape[0]):
        v = zsum[g]
        zpack[0, g] = jnp.where(even, v, 0.0)
        zpack[1, g] = jnp.where(even, 0.0, v)
    zmoves = []
    for i, sz in enumerate((1, -1)):
        copy = pltpu.make_async_remote_copy(
            src_ref=zpack.at[i], dst_ref=zrecv.at[i],
            send_sem=send_sem.at[8 + i], recv_sem=recv_sem.at[8 + i],
            device_id=at(gz=sz), device_id_type=MESH)
        zmoves.append((has["gz", sz], has["gz", -sz], copy))
    for send, _, copy in zmoves:
        pl.when(send)(copy.start)
    for _, receive, copy in zmoves:
        pl.when(receive)(copy.wait_recv)

    def piece(ref, k):
        x, t = divmod(k, tiles)
        return ref[x, t * SUB : (t + 1) * SUB, :]

    def rows(f, carry):
        outer = zrecv[0, f // per] + zrecv[1, f // per]
        outer = pltpu.roll(outer, lax.rem(LANE - (f % per) * (2 * chunks), LANE), 1)
        total = zero
        for k in range(chunks):
            edge = pltpu.roll(outer, LANE - 2 * k, 1) if k else outer
            r = (mid[f, k] + jnp.where(ends, edge, 0.0)) * invden[k]
            s = piece(span_ref, k)
            square = s * s
            gp = jnp.maximum(r, 0.0)
            gm = jnp.maximum(-r, 0.0)
            pp[f, k] = square * (1.001 * gp + 0.001 * gm + RAA)
            qq[f, k] = square * (0.001 * gp + 1.001 * gm + RAA)
            total += s * (1.002 * (gp + gm) + 2 * RAA)
        acc[SUMS - 1 + f] = jnp.where(f > 0, total, zero)
        return carry
    lax.fori_loop(0, FIELDS, rows, 0)
    total = zero
    for k in range(chunks):
        s = piece(span_ref, k)
        square = s * s
        pp[FIELDS, k] = square * (1.001 + RAA)
        qq[FIELDS, k] = square * (0.001 + RAA)
        total += s * (1.002 + 2 * RAA)
    acc[ROWS - 1] = total
    for k in range(FIELDS):
        lam[k] = jnp.full((SUB, LANE), lam0_ref[k], jnp.float32)

    def respond(k, weights):
        big_p, big_q = pp[0, k], qq[0, k]
        for j in range(FIELDS):
            big_p += weights[j] * pp[j + 1, k]
            big_q += weights[j] * qq[j + 1, k]
        s = piece(span_ref, k)
        d = piece(dens_ref, k)
        root_p = jnp.sqrt(big_p)
        root_q = jnp.sqrt(big_q)
        lower, upper = d - s, d + s
        moved = (root_p * lower + root_q * upper) / (root_p + root_q)
        low = jnp.maximum(0.0, d - MOVE * s)
        high = jnp.minimum(1.0, d + MOVE * s)
        return jnp.minimum(jnp.maximum(moved, low), high), big_p, big_q, lower, upper

    def flat(axes):
        index = 0
        for a in axes:
            index = index * shape[a] + me[a]
        return index

    def newton(it, carry):
        weights = [lam[j] for j in range(FIELDS)]
        grads = [zero] * FIELDS
        for k in range(chunks):
            moved, big_p, big_q, lower, upper = respond(k, weights)
            ia = 1.0 / (upper - moved)
            ib = 1.0 / (moved - lower)
            ia2, ib2 = ia * ia, ib * ib
            inv = 1.0 / (2.0 * big_p * (ia2 * ia) + 2.0 * big_q * (ib2 * ib))
            for j in range(FIELDS):
                p, q = pp[j + 1, k], qq[j + 1, k]
                grads[j] += p * ia + q * ib
                a = p * ia2 - q * ib2
                slope[j, k] = a
                scaled[j, k] = a * inv
        for j in range(FIELDS):
            acc[j] = grads[j]
        at_row = FIELDS
        for group in ((0, 1), (2, 3), (4, 5, 6, 7, 8)):
            sums = {(i, j): zero for i in group for j in range(i, FIELDS)}
            for k in range(chunks):
                right = {j: slope[j, k] for j in range(group[0], FIELDS)}
                for i in group:
                    left = scaled[i, k]
                    for j in range(i, FIELDS):
                        sums[i, j] += left * right[j]
            for key in sums:
                acc[at_row] = sums[key]
                at_row += 1

        packed = zero
        for r in range(ROWS):
            packed = jnp.where(lane == r, jnp.sum(acc[r], axis=1, keepdims=True), packed)
        value = jnp.sum(packed, axis=0, keepdims=True)
        for n, axes in enumerate(stages):
            size = math.prod(shape[a] for a in axes)
            part[it, n] = value
            recvs[n][it, flat(axes)] = value
            for o in offsets(axes, shape):
                target = {a: lax.rem(me[a] + d, shape[a]) for a, d in zip(axes, o)}
                pltpu.make_async_remote_copy(
                    src_ref=part.at[it, n], dst_ref=recvs[n].at[it, flat(axes)],
                    send_sem=sum_send.at[it, n], recv_sem=sum_recv.at[it, n],
                    device_id=target, device_id_type=MESH).start()
            whole = recvs[n].at[it, pl.ds(0, size - 1)]
            pltpu.make_async_copy(whole, whole, sum_recv.at[it, n]).wait()
            values = [recvs[n][it, i] for i in range(size)]
            while len(values) > 1:
                values = [sum(values[i + 1 : i + 2], values[i]) for i in range(0, len(values), 2)]
            value = values[0]
        every = jnp.broadcast_to(value, (SUB, LANE))
        for g in range(wide.shape[0]):
            one = jnp.sum(jnp.where(lane == g * SUB + row, every, 0.0), axis=1, keepdims=True)
            wide[g] = jnp.broadcast_to(one, (SUB, LANE))

        def read(r):
            return jnp.broadcast_to(wide[r // SUB, r % SUB : r % SUB + 1, :], (SUB, LANE))
        b = [read(j) - (1.0 - viol_ref[j]) * read(SUMS + j) for j in range(FIELDS)]
        m = {}
        at_row = FIELDS
        for i in range(FIELDS):
            for j in range(i, FIELDS):
                m[i, j] = read(at_row)
                at_row += 1
        trace = m[0, 0]
        for i in range(1, FIELDS):
            trace += m[i, i]
        shift = REG * trace / FIELDS
        for i in range(FIELDS):
            m[i, i] += shift
        inverse = []
        for k in range(FIELDS):
            inverse.append(1.0 / m[k, k])
            for i in range(k + 1, FIELDS):
                factor = m[k, i] * inverse[k]
                for j in range(i, FIELDS):
                    m[i, j] -= factor * m[k, j]
                b[i] -= factor * b[k]
        delta = [None] * FIELDS
        for k in reversed(range(FIELDS)):
            v = b[k]
            for j in range(k + 1, FIELDS):
                v -= m[k, j] * delta[j]
            delta[k] = v * inverse[k]
        for k in range(FIELDS):
            lam[k] = jnp.maximum(weights[k] + delta[k], FLOOR * weights[k])
        return carry
    lax.fori_loop(0, ITERS, newton, 0)

    weights = [lam[j] for j in range(FIELDS)]
    for k in range(chunks):
        x, t = divmod(k, tiles)
        out_ref[x, t * SUB : (t + 1) * SUB, :] = respond(k, weights)[0]
    for j in range(FIELDS):
        lam_out[j] = jnp.max(weights[j])

    for send, _, copy in moves + zmoves:
        pl.when(send)(copy.wait_send)
    for it in range(ITERS):
        for n, axes in enumerate(stages):
            size = math.prod(shape[a] for a in axes)
            whole = recvs[n].at[it, pl.ds(0, size - 1)]
            pltpu.make_async_copy(whole, whole, sum_send.at[it, n]).wait()


def shards(shape, density, spread, sensitivities, violation, multipliers_start):
    nx, ny, nz = density.shape
    chunks = nx * ny // SUB
    per = LANE // (2 * chunks)
    groups = -(-FIELDS // per)
    stages = plan(shape)
    f32 = jnp.float32
    vmem = pl.BlockSpec(memory_space=pltpu.VMEM)
    smem = pl.BlockSpec(memory_space=pltpu.SMEM)
    dma = pltpu.SemaphoreType.DMA
    return pl.pallas_call(
        functools.partial(body, shape, (nx, ny, nz)),
        out_shape=(
            jax.ShapeDtypeStruct((nx, ny, nz), f32),
            jax.ShapeDtypeStruct((FIELDS,), f32),
        ),
        in_specs=[vmem, vmem, pl.BlockSpec(memory_space=pl.ANY), smem, smem],
        out_specs=(vmem, smem),
        scratch_shapes=[
            pltpu.VMEM((FIELDS, nx + 2, ny + 2 * SUB, nz), f32),
            pltpu.VMEM((2, FIELDS, nx, nz), f32),
            pltpu.VMEM((2, FIELDS, nx, nz), f32),
            pltpu.VMEM((4, FIELDS, 1, nz), f32),
            pltpu.VMEM((4, FIELDS, 1, nz), f32),
            pltpu.VMEM((groups, SUB, LANE), f32),
            pltpu.VMEM((2, groups, SUB, LANE), f32),
            pltpu.VMEM((2, groups, SUB, LANE), f32),
            pltpu.VMEM((FIELDS, chunks, SUB, LANE), f32),
            pltpu.VMEM((chunks, SUB, LANE), f32),
            pltpu.VMEM((FIELDS + 1, chunks, SUB, LANE), f32),
            pltpu.VMEM((FIELDS + 1, chunks, SUB, LANE), f32),
            pltpu.VMEM((FIELDS, chunks, SUB, LANE), f32),
            pltpu.VMEM((FIELDS, chunks, SUB, LANE), f32),
            pltpu.VMEM((ROWS, SUB, LANE), f32),
            pltpu.VMEM((-(-ROWS // SUB), SUB, LANE), f32),
            pltpu.VMEM((FIELDS, SUB, LANE), f32),
            pltpu.VMEM((ITERS, len(stages), 1, LANE), f32),
        ] + [
            pltpu.VMEM((ITERS, math.prod(shape[a] for a in axes), 1, LANE), f32) for axes in stages
        ] + [
            dma, dma((10,)), dma((10,)), dma((ITERS, len(stages))), dma((ITERS, len(stages))),
        ],
        compiler_params=pltpu.CompilerParams(collective_id=0, has_side_effects=True),
        name="design_step",
    )(density, spread, sensitivities, violation, multipliers_start)


def solution(mesh):
    shape = {a: int(mesh.shape[a]) for a in AXES}
    return jax.shard_map(
        functools.partial(shards, shape),
        mesh=mesh,
        in_specs=(P("gx", "gy", "gz"), P("gx", "gy", "gz"), P(None, "gx", "gy", "gz"), P(), P()),
        out_specs=(P("gx", "gy", "gz"), P()),
        check_vma=False,
    )
```

time: 188 us -> 37.6 us (0.20)
  blocking collectives: 120 us -> 0 us
  Pallas kernels: 0 us -> 34.8 us
  other arithmetic: 21.8 us -> 0 us
  starting transfers between devices: 13.7 us -> 0 us
  waiting for transfers between devices: 12.4 us -> 0 us
  matrix products: 11 us -> 0 us
  local copies, waits for them, and re-layouts: 5.18 us -> 1.99 us
  between operations: 3.06 us -> 0.65 us
    psum x3 -> x0, blocking collectives: 120 us -> none  [totals(): return lax.psum((gradient_part, schur_part), ('gz', 'gy', 'gx'))]
    pallas_call x0 -> x1, Pallas kernels: none -> 34.8 us  [shards(): pl.pallas_call(functools.partial(body, shape, (nx, ny, nz)), out_shape=(j...]
    ppermute x6 -> x0, starting transfers between devices: 13.7 us -> none  [the longest x3 9.67 us: padded_2(): lax.ppermute(lax.slice_in_dim(block, block.shape[dim] - width, None, axis...]
    ppermute x6 -> x0, waiting for transfers between devices: 12.4 us -> none  [the longest x3 11.1 us: padded_2(): lax.ppermute(lax.slice_in_dim(block, 0, width, axis=dim), axis, backward)]
    dot_general x11 -> x0, matrix products: 10.2 us -> none  [the longest x3 5.02 us: shards(): jnp.dot(slopes / curv, slopes.T, precision=lax.Precision.HIGHEST)]
    another operation x15 -> x0, other arithmetic: 8.48 us -> none  [the longest x9 4.45 us: shards(): factor = jnp.linalg.cholesky(system)]
    reduce_sum x6 -> x0, other arithmetic: 3.57 us -> none  [the longest x3 1.81 us: shards(): shift = REG * jnp.trace(schur) / FIELDS]
    concatenate x5 -> x0, other arithmetic: 3.35 us -> none  [the longest x2 3.11 us: padded_2(): block = jnp.concatenate([low, block, high], axis=dim)]
  transfers between devices with their start and end apart: 6 -> 0, of which waited for: 4 -> 0; matrix products, arithmetic and copies ran while one was open for 2% -> 0% of each run, Pallas kernels for 0% -> 0%
where the time goes in v1:
time: 37.6 us; the launch traced here: 37.4 us
  Pallas kernels  34.8 us (93%)
  local copies, waits for them, and re-layouts  1.99 us (5%)
  between operations  0.65 us (2%)
    pallas_call x1, Pallas kernels, shards(): pl.pallas_call(functools.partial(body, shape, (nx, ny, nz)), out_shape=(j...  34.8 us
    unnamed x4, local copies, waits for them, and re-layouts  1.99 us

profile of v1, /device:TPU:0, one launch (start us, length us, event | category | flops | bytes accessed | tf_op | source)
XLA Modules:
  0.0 37.4 jit_solution(14249576133504624280)
XLA Ops:
  0.6 34.8 %design_step.1 = (f32[8,16,128]{2,1,0:T(8,128)}, f32[9]{0:T(128)}) custom-call(f32[8,16,128]{2,1,0:T(8,128)} %dens_ref.1, f32[8,16,128]{2,1,0:T(8,128)} %span_ref.1, f32[9,8,16,128]{3,2,1,0:T(8,128)} %sens_ref.1, f32[9]{0:T(128)} %viol_ref.1, f32[9]{0:T(128)} %lam0_ref.1), custom_call_target="tpu_custom_call" | custom-call | tf_op jit(solution)/shard_map/design_step/pallas_call | solution.py:382
  35.4 0.0 copy-start
  35.4 1.5 %copy.9 = f32[8,16,128]{2,1,0:T(8,128)} copy(f32[8,16,128]{2,1,0:T(8,128)} %get-tuple-element.4) | data formatting | bytes 131072
  36.9 0.0 copy-done
  36.9 0.5 %copy.10 = f32[9]{0:T(128)} copy(f32[9]{0:T(128)S(1)} %copy-done) | data formatting | bytes 72
Async XLA Ops:
  35.4 1.5 %copy-start = (f32[9]{0:T(128)S(1)}, f32[9]{0:T(128)}, u32[]{:S(2)}) copy-start(f32[9]{0:T(128)} %get-tuple-element.5) | copy-start | bytes 112

commit v2 on v1

--- a/solution.py
+++ b/solution.py
@@ -27,6 +27,7 @@
 SUMS = FIELDS + FIELDS * (FIELDS + 1) // 2
 ROWS = SUMS + FIELDS
 MESH = pl.DeviceIdType.MESH
+GROUP = 3
 
 
 def plan(shape):
@@ -43,42 +44,71 @@
     return [o for o in out if any(o)]
 
 
-def body(shape, dims, dens_ref, span_ref, sens_ref, viol_ref, lam0_ref, out_ref, lam_out,
-         pad, ypack, yrecv, cpack, crecv, zsum, zpack, zrecv, mid, invden, pp, qq, slope, scaled,
+def steps():
+    return [range(f, min(f + GROUP, FIELDS)) for f in range(0, FIELDS, GROUP)]
+
+
+def body(shape, dims, dens_hbm, span_hbm, sens_ref, viol_hbm, lam0_hbm, out_hbm, lam_out,
+         dens_ref, span_ref, out_ref, viol_ref, lam0_ref, pad, ypack, yrecv, cpack, crecv, zpack, zrecv, mid, invden, pp, qq, slope, scaled,
          acc, wide, lam, part, *rest):
     stages = plan(shape)
     recvs = rest[: len(stages)]
-    load_sem, send_sem, recv_sem, sum_send, sum_recv = rest[len(stages):]
+    load_sem, send_sem, recv_sem, sum_send, sum_recv, known = rest[len(stages):]
     nx, ny, nz = dims
     tiles = ny // SUB
     chunks = nx * tiles
     me = {a: lax.axis_index(a) for a in AXES}
 
-    load = pltpu.make_async_copy(
-        sens_ref, pad.at[:, 1 : nx + 1, SUB : SUB + ny, :], load_sem
-    )
-    load.start()
-
-    partners = set()
-    for axes in stages:
-        for o in offsets(axes, shape):
-            partners.add(tuple(dict(zip(axes, o)).get(a, 0) for a in AXES))
-    for dz, dy, dx in [(dz, 0, 0) for dz in (-1, 1)] + [
-        (0, dy, dx) for dy in (-1, 0, 1) for dx in (-1, 0, 1)
-    ]:
-        o = tuple(d % shape[a] for a, d in zip(AXES, (dz, dy, dx)))
-        if any(o):
-            partners.add(o)
-    partners = sorted(partners)
-    barrier = pltpu.get_barrier_semaphore()
-    for o in partners:
-        target = {a: lax.rem(me[a] + d, shape[a]) for a, d in zip(AXES, o)}
-        pl.semaphore_signal(barrier, inc=1, device_id=target, device_id_type=MESH)
-
     has = {}
     for a in AXES:
         has[a, -1] = me[a] > 0
+        has[a, 0] = jnp.bool_(True)
         has[a, 1] = me[a] < shape[a] - 1
+
+    def both(o):
+        moved = [has[a, d] for a, d in zip(AXES, o) if d]
+        return functools.reduce(jnp.logical_and, moved)
+
+    def at(**moves):
+        return {a: me[a] + d for a, d in moves.items()}
+
+    plane = [(0, dy, dx) for dy in (-1, 0, 1) for dx in (-1, 0, 1) if dy or dx]
+    barrier = pltpu.get_barrier_semaphore()
+    near = shape["gz"] == 2 and shape["gy"] <= 4 and shape["gx"] <= 4
+    if near:
+        greeted = [(-1, 0, 0), (1, 0, 0)] + plane
+        for o in greeted:
+            @pl.when(both(o))
+            def _(o=o):
+                pl.semaphore_signal(barrier, inc=1, device_id=at(gz=o[0], gy=o[1], gx=o[2]),
+                                    device_id_type=MESH)
+        arrivals = sum(both(o).astype(jnp.int32) for o in greeted)
+    else:
+        partners = set()
+        for axes in stages:
+            for o in offsets(axes, shape):
+                partners.add(tuple(dict(zip(axes, o)).get(a, 0) for a in AXES))
+        for d in [(-1, 0, 0), (1, 0, 0)] + plane:
+            o = tuple(d % shape[a] for a, d in zip(AXES, d))
+            if any(o):
+                partners.add(o)
+        partners = sorted(partners)
+        for o in partners:
+            target = {a: lax.rem(me[a] + d, shape[a]) for a, d in zip(AXES, o)}
+            pl.semaphore_signal(barrier, inc=1, device_id=target, device_id_type=MESH)
+        arrivals = len(partners)
+
+    load = pltpu.make_async_copy(
+        sens_ref, pad.at[:, 1 : nx + 1, SUB : SUB + ny, :], load_sem.at[0]
+    )
+    load.start()
+    small = [
+        pltpu.make_async_copy(src, dst, load_sem.at[1 + i])
+        for i, (src, dst) in enumerate([
+            (span_hbm, span_ref), (dens_hbm, dens_ref), (viol_hbm, viol_ref), (lam0_hbm, lam0_ref)])
+    ]
+    for copy in small:
+        copy.start()
 
     lane = lax.broadcasted_iota(jnp.int32, (SUB, LANE), 1)
     row = lax.broadcasted_iota(jnp.int32, (SUB, LANE), 0)
@@ -101,7 +131,6 @@
         @pl.when(jnp.logical_not(jnp.logical_and(has["gx", -sx], has["gy", -sy])))
         def _(i=i):
             crecv[i] = jnp.zeros((FIELDS, 1, LANE), jnp.float32)
-    zsum[...] = jnp.zeros(zsum.shape, jnp.float32)
 
     def count(a, index, extent):
         low = jnp.where(jnp.logical_and(me[a] == 0, index == 0), 0.0, 1.0)
@@ -118,7 +147,7 @@
 
     load.wait()
 
-    def gather(f, carry):
+    for f in range(FIELDS):
         for i, y in enumerate((SUB + ny - 1, SUB)):
             for x in range(nx):
                 ypack[i, f, x : x + 1, :] = pad[f, x + 1, y : y + 1, :]
@@ -126,43 +155,59 @@
             x = nx if sx > 0 else 1
             y = SUB + ny - 1 if sy > 0 else SUB
             cpack[i, f] = pad[f, x, y : y + 1, :]
-        return carry
-    lax.fori_loop(0, FIELDS, gather, 0)
-
-    pl.semaphore_wait(barrier, len(partners))
-
-    def at(**moves):
-        return {a: me[a] + d for a, d in moves.items()}
-
-    moves = []
-    for i, sx in enumerate((1, -1)):
-        copy = pltpu.make_async_remote_copy(
-            src_ref=pad.at[:, nx if sx > 0 else 1, SUB : SUB + ny, :],
-            dst_ref=pad.at[:, 0 if sx > 0 else nx + 1, SUB : SUB + ny, :],
-            send_sem=send_sem.at[i], recv_sem=recv_sem.at[i],
-            device_id=at(gx=sx), device_id_type=MESH)
-        moves.append((has["gx", sx], has["gx", -sx], copy))
+
+    pl.semaphore_wait(barrier, arrivals)
+
+    groups = steps()
+    count_of = len(groups)
+
+    def moves_x(g):
+        fields = pl.ds(groups[g][0], len(groups[g]))
+        out = []
+        for i, sx in enumerate((1, -1)):
+            copy = pltpu.make_async_remote_copy(
+                src_ref=pad.at[fields, nx if sx > 0 else 1, SUB : SUB + ny, :],
+                dst_ref=pad.at[fields, 0 if sx > 0 else nx + 1, SUB : SUB + ny, :],
+                send_sem=send_sem.at[6 + 4 * g + i], recv_sem=recv_sem.at[6 + 4 * g + i],
+                device_id=at(gx=sx), device_id_type=MESH)
+            out.append((has["gx", sx], has["gx", -sx], copy))
+        return out
+
+    moves_c, moves_y, moves_z = [], [], []
     for i, (sx, sy) in enumerate(corners):
         copy = pltpu.make_async_remote_copy(
             src_ref=cpack.at[i], dst_ref=crecv.at[i],
-            send_sem=send_sem.at[4 + i], recv_sem=recv_sem.at[4 + i],
+            send_sem=send_sem.at[2 + i], recv_sem=recv_sem.at[2 + i],
             device_id=at(gx=sx, gy=sy), device_id_type=MESH)
-        moves.append((jnp.logical_and(has["gx", sx], has["gy", sy]),
-                      jnp.logical_and(has["gx", -sx], has["gy", -sy]), copy))
+        moves_c.append((jnp.logical_and(has["gx", sx], has["gy", sy]),
+                        jnp.logical_and(has["gx", -sx], has["gy", -sy]), copy))
     for i, sy in enumerate((1, -1)):
         copy = pltpu.make_async_remote_copy(
             src_ref=ypack.at[i], dst_ref=yrecv.at[i],
-            send_sem=send_sem.at[2 + i], recv_sem=recv_sem.at[2 + i],
+            send_sem=send_sem.at[i], recv_sem=recv_sem.at[i],
             device_id=at(gy=sy), device_id_type=MESH)
-        moves.append((has["gy", sy], has["gy", -sy], copy))
-    for send, _, copy in moves:
-        pl.when(send)(copy.start)
-    for _, receive, copy in moves:
-        pl.when(receive)(copy.wait_recv)
+        moves_y.append((has["gy", sy], has["gy", -sy], copy))
+
+    def start(moves):
+        for send, _, copy in moves:
+            pl.when(send)(copy.start)
+
+    def receive(moves):
+        for _, expected, copy in moves:
+            pl.when(expected)(copy.wait_recv)
+
+    xs = [moves_x(g) for g in range(count_of)]
+    start(moves_c)
+    start(xs[0])
+    start(moves_y)
+    for g in range(1, count_of):
+        start(xs[g])
+    receive(moves_c)
+    receive(moves_y)
 
     ends = jnp.logical_or(lane == 0, lane == LANE - 1)
 
-    def smooth(f, carry):
+    def smooth(f, g):
         for i, y in enumerate((SUB - 1, SUB + ny)):
             for x in range(nx):
                 pad[f, x + 1, y : y + 1, :] = yrecv[i, f, x : x + 1, :]
@@ -189,38 +234,38 @@
                     edge = pltpu.roll(edge, 2 * k, 1)
                 here = jnp.logical_or(lane == 2 * k, lane == (2 * k - 1) % LANE)
                 packed = jnp.where(here, edge, packed)
-        zsum[f // per] += pltpu.roll(packed, (f % per) * (2 * chunks), 1)
-        return carry
-    per = LANE // (2 * chunks)
-    lax.fori_loop(0, FIELDS, smooth, 0)
+        shift = (f - groups[g][0]) * (2 * chunks)
+        return pltpu.roll(packed, shift, 1) if shift else packed
 
     even = (lane % 2) == 0
-    for g in range(zsum.shape[0]):
-        v = zsum[g]
+    for g in range(count_of):
+        receive(xs[g])
+        v = zero
+        for f in groups[g]:
+            v += smooth(f, g)
         zpack[0, g] = jnp.where(even, v, 0.0)
         zpack[1, g] = jnp.where(even, 0.0, v)
-    zmoves = []
-    for i, sz in enumerate((1, -1)):
-        copy = pltpu.make_async_remote_copy(
-            src_ref=zpack.at[i], dst_ref=zrecv.at[i],
-            send_sem=send_sem.at[8 + i], recv_sem=recv_sem.at[8 + i],
-            device_id=at(gz=sz), device_id_type=MESH)
-        zmoves.append((has["gz", sz], has["gz", -sz], copy))
-    for send, _, copy in zmoves:
-        pl.when(send)(copy.start)
-    for _, receive, copy in zmoves:
-        pl.when(receive)(copy.wait_recv)
+        zs = []
+        for i, sz in enumerate((1, -1)):
+            copy = pltpu.make_async_remote_copy(
+                src_ref=zpack.at[i, g], dst_ref=zrecv.at[i, g],
+                send_sem=send_sem.at[8 + 4 * g + i], recv_sem=recv_sem.at[8 + 4 * g + i],
+                device_id=at(gz=sz), device_id_type=MESH)
+            zs.append((has["gz", sz], has["gz", -sz], copy))
+        start(zs)
+        moves_z.append(zs)
 
     def piece(ref, k):
         x, t = divmod(k, tiles)
         return ref[x, t * SUB : (t + 1) * SUB, :]
 
-    def rows(f, carry):
-        outer = zrecv[0, f // per] + zrecv[1, f // per]
-        outer = pltpu.roll(outer, lax.rem(LANE - (f % per) * (2 * chunks), LANE), 1)
+    def rows(f, g):
+        outer = zrecv[0, g] + zrecv[1, g]
+        shift = (f - groups[g][0]) * (2 * chunks)
         total = zero
         for k in range(chunks):
-            edge = pltpu.roll(outer, LANE - 2 * k, 1) if k else outer
+            turn = (LANE - shift - 2 * k) % LANE
+            edge = pltpu.roll(outer, turn, 1) if turn else outer
             r = (mid[f, k] + jnp.where(ends, edge, 0.0)) * invden[k]
             s = piece(span_ref, k)
             square = s * s
@@ -229,9 +274,21 @@
             pp[f, k] = square * (1.001 * gp + 0.001 * gm + RAA)
             qq[f, k] = square * (0.001 * gp + 1.001 * gm + RAA)
             total += s * (1.002 * (gp + gm) + 2 * RAA)
-        acc[SUMS - 1 + f] = jnp.where(f > 0, total, zero)
-        return carry
-    lax.fori_loop(0, FIELDS, rows, 0)
+        if f:
+            acc[SUMS - 1 + f] = total
+
+    for copy in small:
+        copy.wait()
+    for g in range(count_of):
+        receive(moves_z[g])
+        if near and g == 0:
+            for o in plane:
+                @pl.when(both(o))
+                def _(o=o):
+                    pl.semaphore_signal(known, inc=1, device_id=at(gy=o[1], gx=o[2]),
+                                        device_id_type=MESH)
+        for f in groups[g]:
+            rows(f, g)
     total = zero
     for k in range(chunks):
         s = piece(span_ref, k)
@@ -351,49 +408,68 @@
         for k in range(FIELDS):
             lam[k] = jnp.maximum(weights[k] + delta[k], FLOOR * weights[k])
         return carry
+    if near:
+        pl.semaphore_wait(known, sum(both(o).astype(jnp.int32) for o in plane))
     lax.fori_loop(0, ITERS, newton, 0)
 
     weights = [lam[j] for j in range(FIELDS)]
     for k in range(chunks):
         x, t = divmod(k, tiles)
         out_ref[x, t * SUB : (t + 1) * SUB, :] = respond(k, weights)[0]
+    result = pltpu.make_async_copy(out_ref, out_hbm, load_sem.at[0])
+    result.start()
     for j in range(FIELDS):
         lam_out[j] = jnp.max(weights[j])
 
-    for send, _, copy in moves + zmoves:
-        pl.when(send)(copy.wait_send)
+    for moves in [moves_c, moves_y] + xs + moves_z:
+        for send, _, copy in moves:
+            pl.when(send)(copy.wait_send)
     for it in range(ITERS):
         for n, axes in enumerate(stages):
             size = math.prod(shape[a] for a in axes)
             whole = recvs[n].at[it, pl.ds(0, size - 1)]
             pltpu.make_async_copy(whole, whole, sum_send.at[it, n]).wait()
+    result.wait()
+
+
+def finish(field_ref, lam_ref, field_out, lam_out, sem):
+    copies = [pltpu.make_async_copy(field_ref, field_out, sem.at[0]),
+              pltpu.make_async_copy(lam_ref, lam_out, sem.at[1])]
+    for copy in copies:
+        copy.start()
+    for copy in copies:
+        copy.wait()
 
 
 def shards(shape, density, spread, sensitivities, violation, multipliers_start):
     nx, ny, nz = density.shape
     chunks = nx * ny // SUB
-    per = LANE // (2 * chunks)
-    groups = -(-FIELDS // per)
+    groups = len(steps())
     stages = plan(shape)
     f32 = jnp.float32
-    vmem = pl.BlockSpec(memory_space=pltpu.VMEM)
     smem = pl.BlockSpec(memory_space=pltpu.SMEM)
     dma = pltpu.SemaphoreType.DMA
-    return pl.pallas_call(
+    hbm = pl.BlockSpec(memory_space=pltpu.HBM)
+    anywhere = pl.BlockSpec(memory_space=pl.ANY)
+    field, lam = pl.pallas_call(
         functools.partial(body, shape, (nx, ny, nz)),
         out_shape=(
             jax.ShapeDtypeStruct((nx, ny, nz), f32),
             jax.ShapeDtypeStruct((FIELDS,), f32),
         ),
-        in_specs=[vmem, vmem, pl.BlockSpec(memory_space=pl.ANY), smem, smem],
-        out_specs=(vmem, smem),
+        in_specs=[hbm] * 5,
+        out_specs=(anywhere, smem),
         scratch_shapes=[
+            pltpu.VMEM((nx, ny, nz), f32),
+            pltpu.VMEM((nx, ny, nz), f32),
+            pltpu.VMEM((nx, ny, nz), f32),
+            pltpu.SMEM((FIELDS,), f32),
+            pltpu.SMEM((FIELDS,), f32),
             pltpu.VMEM((FIELDS, nx + 2, ny + 2 * SUB, nz), f32),
             pltpu.VMEM((2, FIELDS, nx, nz), f32),
             pltpu.VMEM((2, FIELDS, nx, nz), f32),
             pltpu.VMEM((4, FIELDS, 1, nz), f32),
             pltpu.VMEM((4, FIELDS, 1, nz), f32),
-            pltpu.VMEM((groups, SUB, LANE), f32),
             pltpu.VMEM((2, groups, SUB, LANE), f32),
             pltpu.VMEM((2, groups, SUB, LANE), f32),
             pltpu.VMEM((FIELDS, chunks, SUB, LANE), f32),
@@ -409,11 +485,25 @@
         ] + [
             pltpu.VMEM((ITERS, math.prod(shape[a] for a in axes), 1, LANE), f32) for axes in stages
         ] + [
-            dma, dma((10,)), dma((10,)), dma((ITERS, len(stages))), dma((ITERS, len(stages))),
+            dma((5,)), dma((6 + 4 * groups,)), dma((6 + 4 * groups,)),
+            dma((ITERS, len(stages))), dma((ITERS, len(stages))), pltpu.SemaphoreType.REGULAR,
         ],
-        compiler_params=pltpu.CompilerParams(collective_id=0, has_side_effects=True),
+        compiler_params=pltpu.CompilerParams(
+            collective_id=0, has_side_effects=True, vmem_limit_bytes=24 << 20),
         name="design_step",
-    )(density, spread, sensitivities, violation, multipliers_start)
+    )(*[pltpu.with_memory_space_constraint(v, pltpu.HBM) for v in (density, spread, sensitivities, violation, multipliers_start)])
+    return pl.pallas_call(
+        finish,
+        out_shape=(
+            jax.ShapeDtypeStruct((nx, ny, nz), f32),
+            jax.ShapeDtypeStruct((FIELDS,), f32),
+        ),
+        in_specs=[anywhere, anywhere],
+        out_specs=(hbm, hbm),
+        scratch_shapes=[dma((2,))],
+        compiler_params=pltpu.CompilerParams(vmem_limit_bytes=1 << 20),
+        name="finish",
+    )(field, lam)
 
 
 def solution(mesh):

time: 37.6 us -> 31.1 us (0.83)
  Pallas kernels: 34.8 us -> 30.3 us
  local copies, waits for them, and re-layouts: 1.99 us -> 0 us
    pallas_call x1, Pallas kernels: 34.8 us -> 29.6 us  [shards(): pl.pallas_call(functools.partial(body, shape, (nx, ny, nz)), out_shape=(j...]
    unnamed x4 -> x0, local copies, waits for them, and re-layouts: 1.99 us -> none
    pallas_call x0 -> x1, Pallas kernels: none -> 0.65 us  [shards(): pl.pallas_call(finish, out_shape=(jax.ShapeDtypeStruct((nx, ny, nz), f32)...]
where the time goes in v2:
time: 31.1 us; the launch traced here: 30.9 us
  Pallas kernels  30.3 us (97%)
  between operations  0.64 us (2%)
    pallas_call x1, Pallas kernels, shards(): pl.pallas_call(functools.partial(body, shape, (nx, ny, nz)), out_shape=(j...  29.6 us
    pallas_call x1, Pallas kernels, shards(): pl.pallas_call(finish, out_shape=(jax.ShapeDtypeStruct((nx, ny, nz), f32)...  0.65 us

profile of v2, /device:TPU:0, one launch (start us, length us, event | category | flops | bytes accessed | tf_op | source)
XLA Modules:
  0.0 30.9 jit_solution(9947922713831363120)
XLA Ops:
  0.6 29.6 %design_step.1 = (f32[8,16,128]{2,1,0:T(8,128)S(1)}, f32[9]{0:T(128)S(1)}) custom-call(f32[8,16,128]{2,1,0:T(8,128)} %dens_hbm.1, f32[8,16,128]{2,1,0:T(8,128)} %span_hbm.1, f32[9,8,16,128]{3,2,1,0:T(8,128)} %sens_ref.1, f32[9]{0:T(128)} %viol_hbm.1, f32[9]{0:T(128)} %lam0_hbm.1), custom_call_target="tpu_custom_call" | custom-call | tf_op jit(solution)/shard_map/design_step/pallas_call | solution.py:454
  30.3 0.7 %finish.1 = (f32[8,16,128]{2,1,0:T(8,128)}, f32[9]{0:T(128)}) custom-call(f32[8,16,128]{2,1,0:T(8,128)S(1)} %get-tuple-element.4.field_ref, f32[9]{0:T(128)S(1)} %get-tuple-element.5.lam_ref), custom_call_target="tpu_custom_call" | custom-call | tf_op jit(solution)/shard_map/finish/pallas_call | solution.py:495

commit v3 on v2

--- a/solution.py
+++ b/solution.py
@@ -359,7 +359,7 @@
             size = math.prod(shape[a] for a in axes)
             part[it, n] = value
             recvs[n][it, flat(axes)] = value
-            for o in offsets(axes, shape):
+            for o in sorted(offsets(axes, shape), key=lambda o: (-abs(o[-1] - 2), o), reverse=True):
                 target = {a: lax.rem(me[a] + d, shape[a]) for a, d in zip(axes, o)}
                 pltpu.make_async_remote_copy(
                     src_ref=part.at[it, n], dst_ref=recvs[n].at[it, flat(axes)],

time: 31.1 us -> 30.8 us (level)
  no operation moved by 1% of the time
where the time goes in v3:
time: 30.8 us; the launch traced here: 30.6 us
  Pallas kernels  30 us (97%)
  between operations  0.64 us (2%)
    pallas_call x1, Pallas kernels, shards(): pl.pallas_call(functools.partial(body, shape, (nx, ny, nz)), out_shape=(j...  29.3 us
    pallas_call x1, Pallas kernels, shards(): pl.pallas_call(finish, out_shape=(jax.ShapeDtypeStruct((nx, ny, nz), f32)...  0.65 us

profile of v3, /device:TPU:0, one launch (start us, length us, event | category | flops | bytes accessed | tf_op | source)
XLA Modules:
  0.0 30.6 jit_solution(2572600176714609593)
XLA Ops:
  0.6 29.3 %design_step.1 = (f32[8,16,128]{2,1,0:T(8,128)S(1)}, f32[9]{0:T(128)S(1)}) custom-call(f32[8,16,128]{2,1,0:T(8,128)} %dens_hbm.1, f32[8,16,128]{2,1,0:T(8,128)} %span_hbm.1, f32[9,8,16,128]{3,2,1,0:T(8,128)} %sens_ref.1, f32[9]{0:T(128)} %viol_hbm.1, f32[9]{0:T(128)} %lam0_hbm.1), custom_call_target="tpu_custom_call" | custom-call | tf_op jit(solution)/shard_map/design_step/pallas_call | solution.py:454
  30.0 0.7 %finish.1 = (f32[8,16,128]{2,1,0:T(8,128)}, f32[9]{0:T(128)}) custom-call(f32[8,16,128]{2,1,0:T(8,128)S(1)} %get-tuple-element.4.field_ref, f32[9]{0:T(128)S(1)} %get-tuple-element.5.lam_ref), custom_call_target="tpu_custom_call" | custom-call | tf_op jit(solution)/shard_map/finish/pallas_call | solution.py:495
